TPU v7x, 32 devices: a whole 2x2x4 slice. The times are simulated.
32 devices in a mesh: parts: 2 (over x), row: 16 (over z, y, core).
Axes of the slice: x: 2, y: 2, z: 4, core: 2. Of those that a mesh axis runs over, the one named last changes fastest.
Arguments:
- sigma_top: bfloat16 [4096, 2048], P(('parts', 'row')), parts along dimension 0, may hold values from -2 to 8, as said below
- panel_par: bfloat16 [4096, 1024], P(('parts', 'row')), parts along dimension 0, may hold values from -0.25 to 0.25
- dinv_par: float32 [2048, 1024], P(('parts', 'row')), parts along dimension 0, may hold values from -2 to 8, as said below
- panel_kid_top: bfloat16 [4, 2048, 1024], P('parts', 'row'), parts along dimension 0, may hold values from -0.25 to 0.25
- panel_kid_par: bfloat16 [4, 1024, 1024], P('parts', 'row'), parts along dimension 0, may hold values from -0.375 to 0.375
- dvar_kid: float32 [4, 1024], P('parts'), parts along dimension 0, may hold values from 0.5 to 2
- mask_par: int32 [16, 4], P('parts'), parts along dimension 0, may hold values 0 or 1
- mask_kid_top: int32 [4, 8, 4], P('parts'), parts along dimension 0, may hold values 0 or 1
- mask_kid_par: int32 [4, 4, 4], P('parts'), parts along dimension 0, may hold values 0 or 1
Outputs:
- cross_par: bfloat16 [4096, 1024], P(('parts', 'row')), parts along dimension 0
- sigma_par: bfloat16 [2048, 1024], P(('parts', 'row')), parts along dimension 0
- cross_kid_top: bfloat16 [4, 2048, 1024], P('parts', 'row'), parts along dimension 0
- cross_kid_par: bfloat16 [4, 1024, 1024], P('parts', 'row'), parts along dimension 0
- variance_kid: float32 [4, 1024], P('parts'), parts along dimension 0
There are 2 independent parts, one for each index of `parts`. A program takes and returns all parts, laid end to end along the dimension named above; each array names one. Nothing has to cross between parts.
Inputs may be any that keep to these rules, and one draw needn't show every extreme that they name: `sigma_top`: symmetric positive definite. `dinv_par`: symmetric positive definite.
All inputs are finite; a program needn't handle non-finite values.
Results may differ from a plain program's by a relative error of at most 0.0052.
Values may be sent and summed in bfloat16 or wider, within the bound.
A program may use at most 64 MiB of HBM per device.

v0:
```python
import jax
import jax.numpy as jnp
from jax import lax
from jax.sharding import PartitionSpec as P

BLK = 256


def block_mask(mask, rows, first):
    index = (first + jnp.arange(rows, dtype=jnp.int32)) // BLK
    picker = (index[:, None] == jnp.arange(mask.shape[-2], dtype=jnp.int32)[None, :]).astype(
        jnp.float32
    )
    picked = jnp.einsum("rb,...bc->...rc", picker, mask.astype(jnp.float32))
    return jnp.repeat(picked, BLK, axis=-1).astype(jnp.bfloat16)


def shards(
    sigma_top,
    panel_par,
    dinv_par,
    panel_kid_top,
    panel_kid_par,
    dvar_kid,
    mask_par,
    mask_kid_top,
    mask_kid_par,
):
    rows_top = sigma_top.shape[0]
    rows_par = dinv_par.shape[0]
    position = lax.axis_index("row")
    par_masked = panel_par * block_mask(mask_par, rows_top, position * rows_top)
    kid_top_masked = panel_kid_top * block_mask(mask_kid_top, rows_top, position * rows_top)
    kid_par_masked = panel_kid_par * block_mask(mask_kid_par, rows_par, position * rows_par)
    columns = sigma_top
    cross_wide = jnp.dot(
        columns,
        lax.all_gather(par_masked, "row", axis=0, tiled=True),
        preferred_element_type=jnp.float32,
    )
    cross_par = cross_wide.astype(jnp.bfloat16)
    turned = lax.all_to_all(par_masked, "row", split_axis=1, concat_axis=0, tiled=True)
    panel_rows = turned.T
    columns = panel_rows
    diag_sum = jnp.dot(
        columns,
        lax.all_gather(cross_par, "row", axis=0, tiled=True),
        preferred_element_type=jnp.float32,
    )
    sigma_par = (dinv_par + diag_sum).astype(jnp.bfloat16)
    turned_cross = lax.all_to_all(cross_par, "row", split_axis=1, concat_axis=0, tiled=True)
    cross_rows_par = turned_cross.T
    piece = lax.all_gather(kid_top_masked, "row", axis=1, tiled=True)
    upper = jnp.einsum("rc,kcw->krw", sigma_top, piece, preferred_element_type=jnp.float32)
    lower = jnp.einsum("rc,kcw->krw", cross_rows_par, piece, preferred_element_type=jnp.float32)
    acc_top = upper
    acc_par = lower
    piece = lax.all_gather(kid_par_masked, "row", axis=1, tiled=True)
    upper = acc_top + jnp.einsum(
        "rc,kcw->krw", cross_par, piece, preferred_element_type=jnp.float32
    )
    lower = acc_par + jnp.einsum(
        "rc,kcw->krw", sigma_par, piece, preferred_element_type=jnp.float32
    )
    cross_kid_top = upper.astype(jnp.bfloat16)
    cross_kid_par = lower.astype(jnp.bfloat16)
    partial_var = jnp.sum(
        kid_top_masked.astype(jnp.float32) * cross_kid_top.astype(jnp.float32), axis=1
    )
    partial_var = partial_var + jnp.sum(
        kid_par_masked.astype(jnp.float32) * cross_kid_par.astype(jnp.float32), axis=1
    )
    variance_kid = dvar_kid + lax.psum(partial_var, "row")
    return (cross_par, sigma_par, cross_kid_top, cross_kid_par, variance_kid)


def solution(mesh):
    return jax.shard_map(
        shards,
        mesh=mesh,
        in_specs=(
            P(("parts", "row"), None),
            P(("parts", "row"), None),
            P(("parts", "row"), None),
            P("parts", "row", None),
            P("parts", "row", None),
            P("parts", None),
            P("parts", None),
            P("parts", None, None),
            P("parts", None, None),
        ),
        out_specs=(
            P(("parts", "row"), None),
            P(("parts", "row"), None),
            P("parts", "row", None),
            P("parts", "row", None),
            P("parts", None),
        ),
        check_vma=False,
    )
```

profile of v0, /device:TPU:0, one launch (start us, length us, event | category | flops | bytes accessed | tf_op | source)
XLA Modules:
  0.0 304.0 jit_solution(11202252859310362242)
XLA Ops:
  7.3 1.2 copy.21
  8.4 0.8 convolution_convert_fusion.1
  9.2 0.7 bitcast_multiply_fusion
  10.1 55.9 %all-gather.5.cloned.1.call-done = bf16[2048,1024]{0,1:T(8,128)(2,1)} async-done(((bf16[128,1024]{0,1:T(8,128)(2,1)}), bf16[2048,1024]{0,1:T(8,128)(2,1)}) %all-gather.5.cloned.1.call-update) | async-done | bytes 4194320 | tf_op jit(solution)/shard_map/all_gather | solution.py:38
  66.0 4.1 %convolution_convert_fusion = bf16[1024,128]{1,0:T(8,128)(2,1)} fusion(bf16[2048,1024]{0,1:T(8,128)(2,1)} %all-gather.5.cloned.1.call-done, bf16[128,2048]{1,0:T(8,128)(2,1)S(1)} %copy-done), kind=kOutput, calls=%fused_computation.5 | convolution fusion | flops 537001984 | bytes 4980736 | tf_op jit(solution)/shard_map/dot_general | solution.py:36
  70.2 0.1 fusion.12
  70.3 0.1 copy.23
  70.5 0.3 broadcast_in_dim.7
  70.8 0.4 convert_element_type.81
  71.2 1.0 mul.24
  72.3 0.1 copy.24
  72.4 0.1 fusion.16
  72.6 0.1 copy.25
  72.7 0.2 broadcast_in_dim.8
  72.9 0.2 convert_element_type.85
  73.1 0.8 mul.26
  73.9 16.0 %all_to_all.38 = bf16[128,16,64]{0,2,1:T(8,128)(2,1)S(1)} all-to-all(bf16[128,16,64]{0,2,1:T(8,128)(2,1)S(1)} %bitcast.55), channel_id=1, replica_groups=mesh['parts'=2,'row'=16] {'row'}, dimensions={1} | all-to-all | bytes 524288 | tf_op jit(solution)/shard_map/all_to_all | solution.py:51
  89.9 5.7 %all-to-all-start = ((bf16[128,16,64]{0,2,1:T(8,128)(2,1)}), bf16[128,16,64]{0,2,1:T(8,128)(2,1)S(1)}, u32[]{:S(2)}, u32[]{:S(2)}) async-start(bf16[128,16,64]{0,2,1:T(8,128)(2,1)} %bitcast.2), calls=%async_computation | async-start | bytes 524288 | tf_op jit(solution)/shard_map/all_to_all | solution.py:42
  95.6 0.8 copy.28
  96.5 0.2 copy.27
  96.6 0.1 reshape.66
  96.8 9.4 %all-to-all-done = bf16[128,16,64]{0,2,1:T(8,128)(2,1)S(1)} async-done(((bf16[128,16,64]{0,2,1:T(8,128)(2,1)}), bf16[128,16,64]{0,2,1:T(8,128)(2,1)S(1)}, u32[]{:S(2)}, u32[]{:S(2)}) %all-to-all-start) | async-done | bytes 262176 | tf_op jit(solution)/shard_map/all_to_all | solution.py:42
  106.1 21.0 %all-gather.7.cloned.1.call-done = bf16[2048,1024]{0,1:T(8,128)(2,1)} async-done(((bf16[128,1024]{0,1:T(8,128)(2,1)}), bf16[2048,1024]{0,1:T(8,128)(2,1)}) %all-gather.7.cloned.1.call-update) | async-done | bytes 4194320 | tf_op jit(solution)/shard_map/all_gather | solution.py:47
  127.2 3.6 %fusion.4 = bf16[64,1024]{1,0:T(8,128)(2,1)S(1)} fusion(f32[64,1024]{1,0:T(8,128)S(1)} %copy-done.8, bf16[2048,1024]{0,1:T(8,128)(2,1)} %all-gather.7.cloned.1.call-done, bf16[128,16,64]{0,2,1:T(8,128)(2,1)S(1)} %all-to-all-done), kind=kOutput, calls=%fused_computation.8 | convolution fusion | flops 268566528 | bytes 4849664 | tf_op jit(solution)/shard_map/dot_general | solution.py:45
  130.8 73.5 %all-gather.9.cloned.1.call-done = bf16[2,2048,1024]{2,1,0:T(8,128)(2,1)} async-done(((bf16[2,128,1024]{2,1,0:T(8,128)(2,1)}), bf16[2,2048,1024]{2,1,0:T(8,128)(2,1)}) %all-gather.9.cloned.1.call-update) | async-done | bytes 8388624 | tf_op jit(solution)/shard_map/all_gather | solution.py:53
  204.3 4.6 %fusion.5 = f32[2,1024,128]{1,2,0:T(8,128)S(1)} fusion(bf16[2,2048,1024]{2,1,0:T(8,128)(2,1)} %all-gather.9.cloned.1.call-done, bf16[128,2048]{1,0:T(8,128)(2,1)S(1)} %copy-done), kind=kOutput, calls=%fused_computation.11 | convolution fusion | flops 1073741824 | bytes 9961472 | tf_op jit(solution)/shard_map/rc,kcw->krw/dot_general | solution.py:54
  209.0 46.4 %all-gather.11.cloned.1.call-done = bf16[2,1024,1024]{2,1,0:T(8,128)(2,1)} async-done(((bf16[2,64,1024]{2,1,0:T(8,128)(2,1)}), bf16[2,1024,1024]{2,1,0:T(8,128)(2,1)}) %all-gather.11.cloned.1.call-update) | async-done | bytes 4194320 | tf_op jit(solution)/shard_map/all_gather | solution.py:58
  255.4 3.2 %fusion.10 = f32[2,1024,64]{1,2,0:T(8,128)S(1)} fusion(bf16[2,1024,1024]{2,1,0:T(8,128)(2,1)} %all-gather.11.cloned.1.call-done, bf16[64,1024]{1,0:T(8,128)(2,1)S(1)} %fusion.4), kind=kOutput, calls=%fused_computation.18 | convolution fusion | flops 268435456 | bytes 4849664 | tf_op jit(solution)/shard_map/rc,kcw->krw/dot_general | solution.py:62
  258.6 4.2 %multiply_reduce_fusion = (f32[2,1024]{1,0:T(2,128)S(1)}, bf16[2,128,1024]{2,1,0:T(8,128)(2,1)}) fusion(bf16[2,128,1024]{2,1,0:T(8,128)(2,1)S(1)} %copy-done.2, f32[2,1024,128]{1,2,0:T(8,128)S(1)} %fusion.5, bf16[2,1024,1024]{2,1,0:T(8,128)(2,1)} %all-gather.11.cloned.1.call-done, bf16[1024,128]{1,0:T(8,128)(2,1)S(1)} %copy-done.4), kind=kOutput, calls=%fused_computation.10 | convolution fusion | flops 538441728 | bytes 6561792 | tf_op jit(solution)/shard_map/rc,kcw->krw/dot_general | solution.py:59
  262.8 2.3 multiply_reduce_fusion.1
  265.1 31.7 %psum.7 = f32[2,1024]{1,0:T(2,128)S(1)} all-reduce(f32[2,1024]{1,0:T(2,128)S(1)} %add.58), channel_id=1, replica_groups=mesh['parts'=2,'row'=16] {'row'}, use_global_device_ids=true, to_apply=%region_2.3 | all-reduce | flops 2048 | bytes 16384 | tf_op jit(solution)/shard_map/psum | solution.py:73
  296.8 0.6 add.59
  (39 shorter events, 0.3 us)
Async XLA Ops:
  7.2 58.8 %copy-start = (bf16[128,2048]{1,0:T(8,128)(2,1)S(1)}, bf16[128,2048]{1,0:T(8,128)(2,1)}, u32[]{:S(2)}) copy-start(bf16[128,2048]{1,0:T(8,128)(2,1)} %param.9) | copy-start | bytes 1572868
  7.2 63.0 %copy-start.10 = (s32[2,8,4]{1,2,0:T(4,128)S(1)}, s32[2,8,4]{1,2,0:T(4,128)}, u32[]{:S(2)}) copy-start(s32[2,8,4]{1,2,0:T(4,128)} %param.16) | copy-start | bytes 772
  7.2 58.8 %all-gather.5.cloned.1.call-start = ((), (), s32[]{:S(2)}) async-start(), calls=%async_computation.2 | async-start | bytes 4456448 | tf_op jit(solution)/shard_map/all_gather | solution.py:38
  10.0 61.2 %copy-start.5 = (bf16[2,128,1024]{2,1,0:T(8,128)(2,1)S(1)}, bf16[2,128,1024]{2,1,0:T(8,128)(2,1)}, u32[]{:S(2)}) copy-start(bf16[2,128,1024]{2,1,0:T(8,128)(2,1)} %param.12) | copy-start | bytes 1572868
  10.0 62.3 %copy-start.11 = (s32[2,4,4]{2,1,0:T(4,128)S(1)}, s32[2,4,4]{2,1,0:T(4,128)}, u32[]{:S(2)}) copy-start(s32[2,4,4]{2,1,0:T(4,128)} %param.17) | copy-start | bytes 388
  10.0 63.1 %copy-start.7 = (bf16[2,64,1024]{2,1,0:T(8,128)(2,1)S(1)}, bf16[2,64,1024]{2,1,0:T(8,128)(2,1)}, u32[]{:S(2)}) copy-start(bf16[2,64,1024]{2,1,0:T(8,128)(2,1)} %param.13) | copy-start | bytes 786436
  10.0 117.2 %all-gather.7.cloned.1.call-start = ((), (), s32[]{:S(2)}) async-start(), calls=%async_computation.3 | async-start | bytes 4456448 | tf_op jit(solution)/shard_map/all_gather | solution.py:47
  70.1 3.8 %copy-start.4 = (bf16[1024,128]{1,0:T(8,128)(2,1)S(1)}, bf16[1024,128]{1,0:T(8,128)(2,1)}, u32[]{:S(2)}) copy-start(bf16[1024,128]{1,0:T(8,128)(2,1)} %convolution_convert_fusion) | copy-start | bytes 786436
  70.1 134.2 %all-gather.9.cloned.1.call-start = ((), (), s32[]{:S(2)}) async-start(), calls=%async_computation.4 | async-start | bytes 8912896 | tf_op jit(solution)/shard_map/all_gather | solution.py:53
  70.2 57.0 %copy-start.8 = (f32[64,1024]{1,0:T(8,128)S(1)}, f32[64,1024]{1,0:T(8,128)}, u32[]{:S(2)}) copy-start(f32[64,1024]{1,0:T(8,128)} %param.11) | copy-start | bytes 786436
  72.2 183.1 %all-gather.11.cloned.1.call-start = ((), (), s32[]{:S(2)}) async-start(), calls=%async_computation.5 | async-start | bytes 4456448 | tf_op jit(solution)/shard_map/all_gather | solution.py:58
  89.9 16.3 %all-to-all-start = ((bf16[128,16,64]{0,2,1:T(8,128)(2,1)}), bf16[128,16,64]{0,2,1:T(8,128)(2,1)S(1)}, u32[]{:S(2)}, u32[]{:S(2)}) async-start(bf16[128,16,64]{0,2,1:T(8,128)(2,1)} %bitcast.2), calls=%async_computation | async-start | bytes 524288 | tf_op jit(solution)/shard_map/all_to_all | solution.py:42
  130.8 124.6 %copy-start.6 = (bf16[64,1024]{1,0:T(8,128)(2,1)}, bf16[64,1024]{1,0:T(8,128)(2,1)S(1)}, u32[]{:S(2)}) copy-start(bf16[64,1024]{1,0:T(8,128)(2,1)S(1)} %fusion.4) | copy-start | bytes 393220
  208.9 49.6 %copy-start.2 = (bf16[2,128,1024]{2,1,0:T(8,128)(2,1)S(1)}, bf16[2,128,1024]{2,1,0:T(8,128)(2,1)}, u32[]{:S(2)}) copy-start(bf16[2,128,1024]{2,1,0:T(8,128)(2,1)} %mul.24) | copy-start | bytes 1572868
  255.4 7.4 %copy-start.1 = (bf16[2,2048,1024]{2,1,0:T(8,128)(2,1)S(1)}, bf16[2,2048,1024]{2,1,0:T(8,128)(2,1)}, u32[]{:S(2)}) copy-start(bf16[2,2048,1024]{2,1,0:T(8,128)(2,1)} %all-gather.9.cloned.1.call-done) | copy-start | bytes 25165828
  258.6 4.3 %copy-start.3 = (bf16[2,64,1024]{2,1,0:T(8,128)(2,1)S(1)}, bf16[2,64,1024]{2,1,0:T(8,128)(2,1)}, u32[]{:S(2)}) copy-start(bf16[2,64,1024]{2,1,0:T(8,128)(2,1)} %mul.26) | copy-start | bytes 786436
  262.8 34.0 %copy-start.9 = (f32[2,1024]{1,0:T(2,128)S(1)}, f32[2,1024]{1,0:T(2,128)}, u32[]{:S(2)}) copy-start(f32[2,1024]{1,0:T(2,128)} %param.14) | copy-start | bytes 24580
Sparse Core Ops, SparseCore 0:
  10.7 55.1 all-gather.4
  70.2 56.9 all-gather.6
  130.0 74.2 all-gather.8
  206.3 48.9 all-gather.10
where the time goes:
time: 304 us
  waiting for transfers between devices  206 us (68%)
  blocking collectives  47.7 us (16%)
  matrix products  23.1 us (8%)
  between operations  14 us (5%)
  starting transfers between devices  5.89 us (2%)
  local copies, waits for them, and re-layouts  3.83 us (1%)
  other arithmetic  3.14 us (1%)
    all_gather x1, waiting for transfers between devices, shards(): piece = lax.all_gather(kid_top_masked, 'row', axis=1, tiled=True)  73.5 us
    all_gather x1, waiting for transfers between devices, shards(): lax.all_gather(par_masked, 'row', axis=0, tiled=True)  55.9 us
    all_gather x1, waiting for transfers between devices, shards(): piece = lax.all_gather(kid_par_masked, 'row', axis=1, tiled=True)  46.4 us
    psum x1, blocking collectives, shards(): variance_kid = dvar_kid + lax.psum(partial_var, 'row')  31.7 us
    all_gather x1, waiting for transfers between devices, shards(): lax.all_gather(cross_par, 'row', axis=0, tiled=True)  21 us
    all_to_all x1, blocking collectives, shards(): lax.all_to_all(cross_par, 'row', split_axis=1, concat_axis=0, tiled=True)  16 us
    all_to_all x1, waiting for transfers between devices, shards(): lax.all_to_all(par_masked, 'row', split_axis=1, concat_axis=0, tiled=True)  9.39 us
  transfers between devices with their start and end apart: 5, of which 5 were waited for; matrix products, arithmetic and copies ran while one was open for 4% of the time, Pallas kernels for 0%

commit v1 on v0

--- a/solution.py
+++ b/solution.py
@@ -1,9 +1,16 @@
+import functools
+
 import jax
 import jax.numpy as jnp
 from jax import lax
+from jax.experimental import pallas as pl
+from jax.experimental.pallas import tpu as pltpu
 from jax.sharding import PartitionSpec as P
 
 BLK = 256
+TILE = 256
+MESH = pl.DeviceIdType.MESH
+ACROSS_FIRST = (False, False, False, True)
 
 
 def block_mask(mask, rows, first):
@@ -74,9 +81,352 @@
     return (cross_par, sigma_par, cross_kid_top, cross_kid_par, variance_kid)
 
 
+def fused(
+    n, par, kt, kp, sig, dinv, dvar,
+    o_cross, o_sp, o_ckt, o_ckp, o_var,
+    gpar, gkt, gkp, lhs1, lhs2, acc, ct, part, slots,
+    send_sem, recv_sem, turn_send, turn_recv, var_send, var_recv,
+):
+    me = lax.axis_index("row")
+    c = me % 2
+    b = (me // 2) % 2
+    a = me // 4
+    line = n // 4
+    rows_top = par.shape[0]
+    rows_par = kp.shape[1]
+    wide = par.shape[1]
+    tiles = wide // TILE
+    RIGHT, LEFT, ACROSS, PEER = range(4)
+
+    def at(a_, b_, c_):
+        return (a_ * 2 + b_) * 2 + c_
+
+    targets = (at(a + 1, b, c), at(a - 1, b, c), at(a, 1 - b, c), at(a, b, 1 - c))
+
+    def own(k):
+        return (par, kt.at[0], kp, kt.at[1])[k]
+
+    def slot(k, o):
+        top = pl.ds(pl.multiple_of(o * rows_top, rows_top), rows_top)
+        low = pl.ds(pl.multiple_of(o * rows_par, rows_par), rows_par)
+        if k == 0:
+            return gpar.at[top, :]
+        if k == 2:
+            return gkp.at[:, low, :]
+        return gkt.at[0 if k == 1 else 1, top, :]
+
+    def copy(k, o, way, mine=False):
+        return pltpu.make_async_remote_copy(
+            src_ref=own(k) if mine else slot(k, o),
+            dst_ref=slot(k, o),
+            send_sem=send_sem.at[way, k, o],
+            recv_sem=recv_sem.at[k, o],
+            device_id={"row": targets[way]},
+            device_id_type=MESH,
+        )
+
+    ends = []
+
+    def send(k, o, way, mine=False, cond=None):
+        limit = {RIGHT: a < line - 1, LEFT: a > 0}.get(way)
+        if limit is not None:
+            cond = limit if cond is None else jnp.logical_and(cond, limit)
+
+        def go():
+            copy(k, o, way, mine).start()
+
+        def end():
+            copy(k, o, way, mine).wait_send()
+
+        if cond is None:
+            go()
+            ends.append(end)
+        else:
+            pl.when(cond)(go)
+            ends.append(lambda: pl.when(cond)(end))
+
+    def got(k, o, cond=None):
+        def go():
+            copy(k, o, PEER).wait_recv()
+
+        if cond is None:
+            go()
+        else:
+            pl.when(cond)(go)
+
+    def start_across(k):
+        send(k, me, ACROSS, True)
+
+    def start_line(k):
+        send(k, me, RIGHT, True)
+        send(k, me, LEFT, True)
+        if not ACROSS_FIRST[k]:
+            send(k, me, ACROSS, True)
+        send(k, me, PEER, True)
+
+    def step(k, s, way, b_):
+        o = at(a - s, b_, c) if way == RIGHT else at(a + s, b_, c)
+        cond = a >= s if way == RIGHT else a + s < line
+        got(k, o, cond)
+        send(k, o, way, cond=cond)
+        if not ACROSS_FIRST[k]:
+            send(k, o, ACROSS, cond=cond)
+        send(k, o, PEER, cond=cond)
+
+    def crossed(k, s):
+        for sign in (-1, 1) if s else (1,):
+            o = at(a + sign * s, 1 - b, c)
+            cond = None if s == 0 else (a >= s if sign < 0 else a + s < line)
+            got(k, o, cond)
+            if ACROSS_FIRST[k]:
+                send(k, o, RIGHT, cond=cond)
+                send(k, o, LEFT, cond=cond)
+            send(k, o, PEER, cond=cond)
+
+    def peers(k):
+        for a_ in range(line):
+            for b_ in range(2):
+                got(k, at(a_, b_, 1 - c))
+
+    todo = []
+
+    def work(count=1):
+        for _ in range(count):
+            if todo:
+                todo.pop(0)()
+
+    def cols(t):
+        return pl.ds(t * TILE, TILE)
+
+    def cross_tile(t):
+        wide_sum = jnp.dot(sig[...], gpar[:, cols(t)], preferred_element_type=jnp.float32)
+        value = wide_sum.astype(jnp.bfloat16)
+        o_cross[:, cols(t)] = value
+        lhs2[pl.ds(0, rows_top), cols(t)] = value
+        ct[cols(t), :] = wide_sum.T.astype(jnp.bfloat16)
+
+    def turn(j):
+        return pltpu.make_async_remote_copy(
+            src_ref=ct.at[pl.ds(pl.multiple_of(j * rows_par, rows_par), rows_par), :],
+            dst_ref=lhs1.at[
+                pl.ds(rows_top, rows_par), pl.ds(pl.multiple_of(me * rows_top, rows_top), rows_top)
+            ],
+            send_sem=turn_send.at[j],
+            recv_sem=turn_recv.at[me],
+            device_id={"row": j},
+            device_id_type=MESH,
+        )
+
+    def turn_start():
+        for d in range(1, n):
+            turn((me + d) % n).start()
+        lhs1[pl.ds(rows_top, rows_par), pl.ds(pl.multiple_of(me * rows_top, rows_top), rows_top)] = ct[
+            pl.ds(pl.multiple_of(me * rows_par, rows_par), rows_par), :
+        ]
+
+    def turn_end():
+        for d in range(1, n):
+            o = (me + d) % n
+            here = lhs1.at[
+                pl.ds(rows_top, rows_par), pl.ds(pl.multiple_of(o * rows_top, rows_top), rows_top)
+            ]
+            pltpu.make_async_remote_copy(
+                src_ref=here,
+                dst_ref=here,
+                send_sem=turn_send.at[o],
+                recv_sem=turn_recv.at[o],
+                device_id={"row": o},
+                device_id_type=MESH,
+            ).wait_recv()
+
+    def sigma_tile(t):
+        value = dinv[:, cols(t)] + jnp.dot(
+            lhs1[pl.ds(rows_top, rows_par), :], gpar[:, cols(t)], preferred_element_type=jnp.float32
+        )
+        value = value.astype(jnp.bfloat16)
+        o_sp[:, cols(t)] = value
+        lhs2[pl.ds(rows_top, rows_par), cols(t)] = value
+
+    def low_tile(k, t):
+        total = jnp.dot(lhs2[...], gkp[k, :, cols(t)], preferred_element_type=jnp.float32)
+        acc[k, :, cols(t)] = total
+
+    def top_tile(k, t):
+        return jnp.dot(lhs1[...], gkt[k, :, cols(t)], preferred_element_type=jnp.float32)
+
+    def first_top(t):
+        acc[0, :, cols(t)] = top_tile(0, t)
+
+    def finish(k, t, total):
+        value = (acc[k, :, cols(t)] + total).astype(jnp.bfloat16)
+        o_ckt[k, :, cols(t)] = value[:rows_top]
+        o_ckp[k, :, cols(t)] = value[rows_top:]
+        back = value.astype(jnp.float32)
+        var = jnp.sum(kt[k, :, cols(t)].astype(jnp.float32) * back[:rows_top], axis=0, keepdims=True)
+        var = var + jnp.sum(
+            kp[k, :, cols(t)].astype(jnp.float32) * back[rows_top:], axis=0, keepdims=True
+        )
+        part[pl.ds(k, 1), cols(t)] = var
+
+    def finish_first(t):
+        finish(0, t, jnp.dot(lhs2[...], gkp[0, :, cols(t)], preferred_element_type=jnp.float32))
+
+    barrier = pltpu.get_barrier_semaphore()
+    for d in range(1, n):
+        pl.semaphore_signal(
+            barrier, inc=1, device_id={"row": (me + d) % n}, device_id_type=MESH
+        )
+    pl.semaphore_wait(barrier, n - 1)
+
+    start_line(0)
+    for k in range(4):
+        if ACROSS_FIRST[k]:
+            start_across(k)
+    start_line(1)
+    top = pl.ds(pl.multiple_of(me * rows_top, rows_top), rows_top)
+    low = pl.ds(pl.multiple_of(me * rows_par, rows_par), rows_par)
+    gpar[top, :] = par[...]
+    gkt[:, top, :] = kt[...]
+    gkp[:, low, :] = kp[...]
+    lhs1[pl.ds(0, rows_top), :] = sig[...]
+
+    late = []
+    for k in range(4):
+        if k + 2 < 4:
+            pre = k + 2
+        else:
+            pre = None
+        sides = (b, 1 - b) if ACROSS_FIRST[k] else (b,)
+        if ACROSS_FIRST[k]:
+            crossed(k, 0)
+        for s in range(1, line):
+            for b_ in sides:
+                for way in (RIGHT, LEFT):
+                    step(k, s, way, b_)
+            if s == 1 and pre is not None:
+                start_line(pre)
+            while late:
+                late.pop(0)()
+            if not ACROSS_FIRST[k]:
+                late.append(functools.partial(crossed, k, s - 1))
+            work(4)
+        if not ACROSS_FIRST[k]:
+            late.append(functools.partial(crossed, k, line - 1))
+        if k == 0:
+            todo.append(lambda: (peers(0), cross_tile(0)))
+            todo.extend(functools.partial(cross_tile, t) for t in range(1, tiles))
+            todo.append(turn_start)
+        if k == 1:
+            todo.append(turn_end)
+            todo.extend(functools.partial(sigma_tile, t) for t in range(tiles))
+            todo.append(lambda: (peers(1), first_top(0)))
+            todo.extend(functools.partial(first_top, t) for t in range(1, tiles))
+        if k == 2:
+            todo.append(lambda: (peers(2), finish_first(0)))
+            todo.extend(functools.partial(finish_first, t) for t in range(1, tiles))
+            todo.extend(functools.partial(low_tile, 1, t) for t in range(tiles))
+    while late:
+        late.pop(0)()
+    work(len(todo))
+    peers(3)
+    for t in range(tiles):
+        finish(1, t, top_tile(1, t))
+
+    def var_copy(j, o):
+        return pltpu.make_async_remote_copy(
+            src_ref=part,
+            dst_ref=slots.at[o],
+            send_sem=var_send.at[j],
+            recv_sem=var_recv.at[o],
+            device_id={"row": j},
+            device_id_type=MESH,
+        )
+
+    for d in range(1, n):
+        var_copy((me + d) % n, me).start()
+    slots[me] = part[...]
+    for end in ends:
+        end()
+    for d in range(1, n):
+        turn((me + d) % n).wait_send()
+    for d in range(1, n):
+        other = (me + d) % n
+        var_copy(other, other).wait_recv()
+    total = dvar[...]
+    for o in range(n):
+        total = total + slots[o]
+    o_var[...] = total
+    for d in range(1, n):
+        var_copy((me + d) % n, me).wait_send()
+
+
+def fused_shards(
+    n,
+    sigma_top,
+    panel_par,
+    dinv_par,
+    panel_kid_top,
+    panel_kid_par,
+    dvar_kid,
+    mask_par,
+    mask_kid_top,
+    mask_kid_par,
+):
+    rows_top, width_top = sigma_top.shape
+    rows_par, width_par = dinv_par.shape
+    kids, _, width_kid = panel_kid_top.shape
+    position = lax.axis_index("row")
+    par_masked = panel_par * block_mask(mask_par, rows_top, position * rows_top)
+    kid_top_masked = panel_kid_top * block_mask(mask_kid_top, rows_top, position * rows_top)
+    kid_par_masked = panel_kid_par * block_mask(mask_kid_par, rows_par, position * rows_par)
+    bf16, f32 = jnp.bfloat16, jnp.float32
+    rows = rows_top + rows_par
+    sem = pltpu.SemaphoreType.DMA
+    return pl.pallas_call(
+        functools.partial(fused, n),
+        out_shape=(
+            jax.ShapeDtypeStruct((rows_top, width_par), bf16),
+            jax.ShapeDtypeStruct((rows_par, width_par), bf16),
+            jax.ShapeDtypeStruct((kids, rows_top, width_kid), bf16),
+            jax.ShapeDtypeStruct((kids, rows_par, width_kid), bf16),
+            jax.ShapeDtypeStruct((kids, width_kid), f32),
+        ),
+        in_specs=[pl.BlockSpec(memory_space=pltpu.VMEM)] * 6,
+        out_specs=[pl.BlockSpec(memory_space=pltpu.VMEM)] * 5,
+        scratch_shapes=[
+            pltpu.VMEM((width_top, width_par), bf16),
+            pltpu.VMEM((kids, width_top, width_kid), bf16),
+            pltpu.VMEM((kids, width_par, width_kid), bf16),
+            pltpu.VMEM((rows, width_top), bf16),
+            pltpu.VMEM((rows, width_par), bf16),
+            pltpu.VMEM((kids, rows, width_kid), f32),
+            pltpu.VMEM((width_par, rows_top), bf16),
+            pltpu.VMEM((kids, width_kid), f32),
+            pltpu.VMEM((n, kids, width_kid), f32),
+            sem((4, 4, n)),
+            sem((4, n)),
+            sem((n,)),
+            sem((n,)),
+            sem((n,)),
+            sem((n,)),
+        ],
+        compiler_params=pltpu.CompilerParams(
+            collective_id=0, has_side_effects=True, vmem_limit_bytes=56 * 2**20
+        ),
+        name="fused",
+    )(par_masked, kid_top_masked, kid_par_masked, sigma_top, dinv_par, dvar_kid)
+
+
+def choose(n, *args):
+    rows_top, rows_par, kids = args[0].shape[0], args[2].shape[0], args[3].shape[0]
+    fits = rows_top % 128 == 0 and rows_par % 16 == 0 and n % 4 == 0 and kids == 2
+    fits = fits and args[1].shape[1] % TILE == 0 and args[1].shape[1] == args[3].shape[2]
+    return fused_shards(n, *args) if fits else shards(*args)
+
+
 def solution(mesh):
     return jax.shard_map(
-        shards,
+        functools.partial(choose, mesh.shape["row"]),
         mesh=mesh,
         in_specs=(
             P(("parts", "row"), None),

time: 304 us -> 135 us (0.44)
  waiting for transfers between devices: 206 us -> 0 us
  Pallas kernels: 0 us -> 120 us
  blocking collectives: 47.7 us -> 0 us
  matrix products: 23.1 us -> 0.36 us
  between operations: 14 us -> 0.75 us
  local copies, waits for them, and re-layouts: 3.83 us -> 11.2 us
  starting transfers between devices: 5.89 us -> 0 us
    all_gather x4 -> x0, waiting for transfers between devices: 197 us -> none  [the longest x1 73.5 us: shards(): piece = lax.all_gather(kid_top_masked, 'row', axis=1, tiled=True)]
    pallas_call x0 -> x1, Pallas kernels: none -> 120 us  [fused_shards(): pl.pallas_call(functools.partial(fused, n), out_shape=(jax.ShapeDtypeStru...]
    psum x1 -> x0, blocking collectives: 31.7 us -> none  [shards(): variance_kid = dvar_kid + lax.psum(partial_var, 'row')]
    dot_general x6 -> x0, matrix products: 22.1 us -> none  [the longest x1 4.63 us: shards(): jnp.einsum('rc,kcw->krw', sigma_top, piece, preferred_element_type=jnp.fl...]
    all_to_all x1 -> x0, blocking collectives: 16 us -> none  [shards(): lax.all_to_all(cross_par, 'row', split_axis=1, concat_axis=0, tiled=True)]
    all_to_all x1 -> x0, waiting for transfers between devices: 9.39 us -> none  [shards(): lax.all_to_all(par_masked, 'row', split_axis=1, concat_axis=0, tiled=True)]
    unnamed x26 -> x24, local copies, waits for them, and re-layouts: 2.08 us -> 9.38 us
    all_to_all x1 -> x0, starting transfers between devices: 5.72 us -> none  [shards(): lax.all_to_all(par_masked, 'row', split_axis=1, concat_axis=0, tiled=True)]
  transfers between devices with their start and end apart: 5 -> 0, of which waited for: 5 -> 0; matrix products, arithmetic and copies ran while one was open for 4% -> 0% of each run, Pallas kernels for 0% -> 0%
where the time goes in v1:
time: 135 us
  Pallas kernels  120 us (89%)
  local copies, waits for them, and re-layouts  11.2 us (8%)
  other arithmetic  2.57 us (2%)
    pallas_call x1, Pallas kernels, fused_shards(): pl.pallas_call(functools.partial(fused, n), out_shape=(jax.ShapeDtypeStru...  120 us
    unnamed x24, local copies, waits for them, and re-layouts  9.38 us

profile of v1, /device:TPU:0, one launch (start us, length us, event | category | flops | bytes accessed | tf_op | source)
XLA Modules:
  0.0 135.1 jit_solution(15116270388352761809)
XLA Ops:
  0.6 0.0 copy-start.8
  0.7 0.6 copy-done.8
  1.3 0.1 convolution_convert_fusion
  1.4 0.1 fusion
  1.6 0.7 copy-done.7
  2.3 0.1 copy.16
  2.4 0.1 fusion.4
  2.5 0.1 copy.17
  2.6 0.1 copy.14
  2.8 0.1 copy.15
  2.9 0.2 broadcast_in_dim.6
  3.1 0.0 copy-start.2
  3.2 0.9 copy-done.2
  4.1 0.8 mul.17.par
  4.8 0.2 broadcast_in_dim.8
  5.0 0.0 copy-start.3
  5.1 0.2 convert_element_type.49
  5.2 0.8 copy-done.3
  6.0 0.8 mul.20.kp
  6.8 0.3 broadcast_in_dim.7
  7.1 0.0 copy-start
  7.1 0.4 convert_element_type.45
  7.5 0.7 copy-done
  8.2 1.0 mul.18.kt
  9.1 120.2 %fused.1 = (bf16[128,1024]{1,0:T(8,128)(2,1)}, bf16[64,1024]{1,0:T(8,128)(2,1)}, bf16[2,128,1024]{2,1,0:T(8,128)(2,1)}, bf16[2,64,1024]{2,1,0:T(8,128)(2,1)}, f32[2,1024]{1,0:T(2,128)}) custom-call(bf16[128,1024]{1,0:T(8,128)(2,1)} %mul.17.par, bf16[2,128,1024]{2,1,0:T(8,128)(2,1)} %mul.18.kt, bf16[2,64,1024]{2,1,0:T(8,128)(2,1)} %mul.20.kp, ...), custom_call_target="tpu_custom_call" | custom-call | tf_op jit(solution)/shard_map/fused/pallas_call | solution.py:385
  129.4 1.7 %copy.24 = bf16[128,1024]{1,0:T(8,128)(2,1)} copy(bf16[128,1024]{1,0:T(8,128)(2,1)} %get-tuple-element.10) | data formatting | bytes 524288
  131.1 1.6 %copy.25 = bf16[64,1024]{1,0:T(8,128)(2,1)} copy(bf16[64,1024]{1,0:T(8,128)(2,1)} %get-tuple-element.11) | data formatting | bytes 262144
  132.7 0.8 copy.26
  133.5 0.3 copy-done.4
  133.8 0.7 copy.27
  134.5 0.0 copy-done.5
  134.5 0.6 copy.28
  (14 shorter events, 0.1 us)
Async XLA Ops:
  0.6 0.7 copy-start.8
  0.6 0.8 copy-start.6
  1.6 0.7 copy-start.7
  3.1 1.0 copy-start.2
  5.0 1.0 copy-start.3
  7.1 1.0 copy-start
  129.4 3.3 %copy-start.1 = (bf16[2,128,1024]{2,1,0:T(8,128)(2,1)S(1)}, bf16[2,128,1024]{2,1,0:T(8,128)(2,1)}, u32[]{:S(2)}) copy-start(bf16[2,128,1024]{2,1,0:T(8,128)(2,1)} %get-tuple-element.12) | copy-start | bytes 1572868
  132.7 1.1 copy-start.4
  133.8 0.7 copy-start.5

commit v2 on v1

--- a/solution.py
+++ b/solution.py
@@ -11,6 +11,7 @@
 TILE = 256
 MESH = pl.DeviceIdType.MESH
 ACROSS_FIRST = (False, False, False, True)
+LAG = 5
 
 
 def block_mask(mask, rows, first):
@@ -82,7 +83,7 @@
 
 
 def fused(
-    n, par, kt, kp, sig, dinv, dvar,
+    n, mpar, mkt, mkp, par, kt, kp, sig, dinv, dvar,
     o_cross, o_sp, o_ckt, o_ckp, o_var,
     gpar, gkt, gkp, lhs1, lhs2, acc, ct, part, slots,
     send_sem, recv_sem, turn_send, turn_recv, var_send, var_recv,
@@ -198,8 +199,31 @@
     def cols(t):
         return pl.ds(t * TILE, TILE)
 
+    def masked(values, mask, first, t):
+        count = values.shape[0] // BLK
+        return jnp.concatenate(
+            [
+                values[r * BLK : (r + 1) * BLK]
+                * mask[first + r, t].astype(jnp.float32).astype(jnp.bfloat16)
+                for r in range(count)
+            ],
+            axis=0,
+        )
+
+    blocks_top = gkt.shape[1] // BLK
+    blocks_par = gkp.shape[1] // BLK
+
+    def all_par(t):
+        return masked(gpar[:, cols(t)], mpar, 0, t)
+
+    def all_kt(k, t):
+        return masked(gkt[k, :, cols(t)], mkt, k * blocks_top, t)
+
+    def all_kp(k, t):
+        return masked(gkp[k, :, cols(t)], mkp, k * blocks_par, t)
+
     def cross_tile(t):
-        wide_sum = jnp.dot(sig[...], gpar[:, cols(t)], preferred_element_type=jnp.float32)
+        wide_sum = jnp.dot(sig[...], all_par(t), preferred_element_type=jnp.float32)
         value = wide_sum.astype(jnp.bfloat16)
         o_cross[:, cols(t)] = value
         lhs2[pl.ds(0, rows_top), cols(t)] = value
@@ -241,18 +265,18 @@
 
     def sigma_tile(t):
         value = dinv[:, cols(t)] + jnp.dot(
-            lhs1[pl.ds(rows_top, rows_par), :], gpar[:, cols(t)], preferred_element_type=jnp.float32
+            lhs1[pl.ds(rows_top, rows_par), :], all_par(t), preferred_element_type=jnp.float32
         )
         value = value.astype(jnp.bfloat16)
         o_sp[:, cols(t)] = value
         lhs2[pl.ds(rows_top, rows_par), cols(t)] = value
 
     def low_tile(k, t):
-        total = jnp.dot(lhs2[...], gkp[k, :, cols(t)], preferred_element_type=jnp.float32)
+        total = jnp.dot(lhs2[...], all_kp(k, t), preferred_element_type=jnp.float32)
         acc[k, :, cols(t)] = total
 
     def top_tile(k, t):
-        return jnp.dot(lhs1[...], gkt[k, :, cols(t)], preferred_element_type=jnp.float32)
+        return jnp.dot(lhs1[...], all_kt(k, t), preferred_element_type=jnp.float32)
 
     def first_top(t):
         acc[0, :, cols(t)] = top_tile(0, t)
@@ -262,14 +286,18 @@
         o_ckt[k, :, cols(t)] = value[:rows_top]
         o_ckp[k, :, cols(t)] = value[rows_top:]
         back = value.astype(jnp.float32)
-        var = jnp.sum(kt[k, :, cols(t)].astype(jnp.float32) * back[:rows_top], axis=0, keepdims=True)
-        var = var + jnp.sum(
+        top_part = jnp.sum(
+            kt[k, :, cols(t)].astype(jnp.float32) * back[:rows_top], axis=0, keepdims=True
+        )
+        low_part = jnp.sum(
             kp[k, :, cols(t)].astype(jnp.float32) * back[rows_top:], axis=0, keepdims=True
         )
-        part[pl.ds(k, 1), cols(t)] = var
+        top_on = mkt[k * blocks_top + me * rows_top // BLK, t].astype(jnp.float32)
+        low_on = mkp[k * blocks_par + me * rows_par // BLK, t].astype(jnp.float32)
+        part[pl.ds(k, 1), cols(t)] = top_part * top_on + low_part * low_on
 
     def finish_first(t):
-        finish(0, t, jnp.dot(lhs2[...], gkp[0, :, cols(t)], preferred_element_type=jnp.float32))
+        finish(0, t, jnp.dot(lhs2[...], all_kp(0, t), preferred_element_type=jnp.float32))
 
     barrier = pltpu.get_barrier_semaphore()
     for d in range(1, n):
@@ -290,43 +318,46 @@
     gkp[:, low, :] = kp[...]
     lhs1[pl.ds(0, rows_top), :] = sig[...]
 
-    late = []
-    for k in range(4):
-        if k + 2 < 4:
-            pre = k + 2
-        else:
-            pre = None
-        sides = (b, 1 - b) if ACROSS_FIRST[k] else (b,)
-        if ACROSS_FIRST[k]:
-            crossed(k, 0)
-        for s in range(1, line):
-            for b_ in sides:
-                for way in (RIGHT, LEFT):
-                    step(k, s, way, b_)
-            if s == 1 and pre is not None:
-                start_line(pre)
-            while late:
-                late.pop(0)()
-            if not ACROSS_FIRST[k]:
-                late.append(functools.partial(crossed, k, s - 1))
-            work(4)
-        if not ACROSS_FIRST[k]:
-            late.append(functools.partial(crossed, k, line - 1))
+    def ready(k):
         if k == 0:
             todo.append(lambda: (peers(0), cross_tile(0)))
             todo.extend(functools.partial(cross_tile, t) for t in range(1, tiles))
             todo.append(turn_start)
         if k == 1:
-            todo.append(turn_end)
+            todo.append(lambda: (peers(1), turn_end(), first_top(0)))
+            todo.extend(functools.partial(first_top, t) for t in range(1, tiles))
             todo.extend(functools.partial(sigma_tile, t) for t in range(tiles))
-            todo.append(lambda: (peers(1), first_top(0)))
-            todo.extend(functools.partial(first_top, t) for t in range(1, tiles))
         if k == 2:
             todo.append(lambda: (peers(2), finish_first(0)))
             todo.extend(functools.partial(finish_first, t) for t in range(1, tiles))
             todo.extend(functools.partial(low_tile, 1, t) for t in range(tiles))
-    while late:
-        late.pop(0)()
+
+    late = {}
+    now = 0
+    for k in range(4):
+        sides = (b, 1 - b) if ACROSS_FIRST[k] else (b,)
+        if not ACROSS_FIRST[k]:
+            for s in range(line):
+                late.setdefault(now + s + LAG, []).append((k, s))
+        for s in range(1, line):
+            now += 1
+            for b_ in sides:
+                for way in (RIGHT, LEFT):
+                    step(k, s, way, b_)
+            if s == 1 and k + 2 < 4:
+                start_line(k + 2)
+            if s == 1 and k + 1 < 4 and ACROSS_FIRST[k + 1]:
+                crossed(k + 1, 0)
+            for k_, s_ in late.pop(now, []):
+                crossed(k_, s_)
+                if s_ == line - 1:
+                    ready(k_)
+            work(4)
+    for when in sorted(late):
+        for k_, s_ in late[when]:
+            crossed(k_, s_)
+            if s_ == line - 1:
+                ready(k_)
     work(len(todo))
     peers(3)
     for t in range(tiles):
@@ -375,10 +406,6 @@
     rows_top, width_top = sigma_top.shape
     rows_par, width_par = dinv_par.shape
     kids, _, width_kid = panel_kid_top.shape
-    position = lax.axis_index("row")
-    par_masked = panel_par * block_mask(mask_par, rows_top, position * rows_top)
-    kid_top_masked = panel_kid_top * block_mask(mask_kid_top, rows_top, position * rows_top)
-    kid_par_masked = panel_kid_par * block_mask(mask_kid_par, rows_par, position * rows_par)
     bf16, f32 = jnp.bfloat16, jnp.float32
     rows = rows_top + rows_par
     sem = pltpu.SemaphoreType.DMA
@@ -391,7 +418,8 @@
             jax.ShapeDtypeStruct((kids, rows_par, width_kid), bf16),
             jax.ShapeDtypeStruct((kids, width_kid), f32),
         ),
-        in_specs=[pl.BlockSpec(memory_space=pltpu.VMEM)] * 6,
+        in_specs=[pl.BlockSpec(memory_space=pltpu.SMEM)] * 3
+        + [pl.BlockSpec(memory_space=pltpu.VMEM)] * 6,
         out_specs=[pl.BlockSpec(memory_space=pltpu.VMEM)] * 5,
         scratch_shapes=[
             pltpu.VMEM((width_top, width_par), bf16),
@@ -414,12 +442,23 @@
             collective_id=0, has_side_effects=True, vmem_limit_bytes=56 * 2**20
         ),
         name="fused",
-    )(par_masked, kid_top_masked, kid_par_masked, sigma_top, dinv_par, dvar_kid)
+    )(
+        mask_par,
+        mask_kid_top.reshape(-1, mask_kid_top.shape[-1]),
+        mask_kid_par.reshape(-1, mask_kid_par.shape[-1]),
+        panel_par,
+        panel_kid_top,
+        panel_kid_par,
+        sigma_top,
+        dinv_par,
+        dvar_kid,
+    )
 
 
 def choose(n, *args):
     rows_top, rows_par, kids = args[0].shape[0], args[2].shape[0], args[3].shape[0]
     fits = rows_top % 128 == 0 and rows_par % 16 == 0 and n % 4 == 0 and kids == 2
+    fits = fits and BLK % rows_top == 0 and BLK % rows_par == 0 and TILE == BLK
     fits = fits and args[1].shape[1] % TILE == 0 and args[1].shape[1] == args[3].shape[2]
     return fused_shards(n, *args) if fits else shards(*args)
 

time: 135 us -> 119 us (0.88)
  Pallas kernels: 120 us -> 110 us
  local copies, waits for them, and re-layouts: 11.2 us -> 7.73 us
  other arithmetic: 2.57 us -> 0 us
    pallas_call x1, Pallas kernels: 120 us -> 110 us  [fused_shards(): pl.pallas_call(functools.partial(fused, n), out_shape=(jax.ShapeDtypeStru...]
    mul x3 -> x0, other arithmetic: 2.53 us -> none  [the longest x1 0.99 us: fused_shards(): panel_kid_top * block_mask(mask_kid_top, rows_top, position * rows_top)]
    unnamed x24 -> x14, local copies, waits for them, and re-layouts: 9.38 us -> 7.05 us
where the time goes in v2:
time: 119 us
  Pallas kernels  110 us (92%)
  local copies, waits for them, and re-layouts  7.73 us (6%)
    pallas_call x1, Pallas kernels, fused_shards(): pl.pallas_call(functools.partial(fused, n), out_shape=(jax.ShapeDtypeStru...  110 us
    unnamed x14, local copies, waits for them, and re-layouts  7.05 us

profile of v2, /device:TPU:0, one launch (start us, length us, event | category | flops | bytes accessed | tf_op | source)
XLA Modules:
  0.0 118.9 jit_solution(13684525068011047240)
XLA Ops:
  0.6 0.0 copy-start.3
  0.6 1.4 %copy.16.mpar = s32[8,4]{1,0:T(8,128)} copy(s32[8,4]{0,1:T(4,128)} %param.15) | data formatting | bytes 256 | tf_op args[6]
  2.0 0.0 copy-done.3
  2.0 0.7 copy.19
  2.7 110.5 %fused.1 = (bf16[128,1024]{1,0:T(8,128)(2,1)}, bf16[64,1024]{1,0:T(8,128)(2,1)}, bf16[2,128,1024]{2,1,0:T(8,128)(2,1)}, bf16[2,64,1024]{2,1,0:T(8,128)(2,1)}, f32[2,1024]{1,0:T(2,128)}) custom-call(s32[8,4]{1,0:T(8,128)} %copy.16.mpar, s32[16,4]{1,0:T(8,128)} %bitcast.2, s32[8,4]{1,0:T(8,128)} %bitcast.3, bf16[128,1024]{1,0:T(8,128)(2,1)} %par.1, ...), custom_call_target="tpu_custom_call" | custom-call | tf_op jit(solution)/shard_map/fused/pallas_call | solution.py:412
  113.2 0.0 copy-start
  113.2 1.7 %copy.27 = bf16[128,1024]{1,0:T(8,128)(2,1)} copy(bf16[128,1024]{1,0:T(8,128)(2,1)} %get-tuple-element.10) | data formatting | bytes 524288
  114.9 1.6 %copy.28 = bf16[64,1024]{1,0:T(8,128)(2,1)} copy(bf16[64,1024]{1,0:T(8,128)(2,1)} %get-tuple-element.11) | data formatting | bytes 262144
  116.5 0.0 copy-done
  116.5 0.0 copy-start.1
  116.5 0.8 copy.29
  117.3 0.3 copy-done.1
  117.6 0.0 copy-start.2
  117.6 0.7 copy.30
  118.3 0.0 copy-done.2
  118.3 0.6 copy.31
Async XLA Ops:
  0.6 1.4 %copy-start.3 = (s32[2,8,4]{1,2,0:T(4,128)S(1)}, s32[2,8,4]{1,2,0:T(4,128)}, u32[]{:S(2)}) copy-start(s32[2,8,4]{1,2,0:T(4,128)} %param.16) | copy-start | bytes 772
  113.2 3.3 %copy-start = (bf16[2,128,1024]{2,1,0:T(8,128)(2,1)S(1)}, bf16[2,128,1024]{2,1,0:T(8,128)(2,1)}, u32[]{:S(2)}) copy-start(bf16[2,128,1024]{2,1,0:T(8,128)(2,1)} %get-tuple-element.12) | copy-start | bytes 1572868
  116.5 1.1 copy-start.1
  117.6 0.7 copy-start.2
